TPU v7x, 128 devices: a whole 4x4x4 slice. The times are simulated.
128 devices in a mesh: row: 8 (over y, z_lo), col: 16 (over x, z_hi, core).
Axes of the slice: x: 4, y: 4, z: 4 (z_hi: 2, z_lo: 2; z = z_hi * 2 + z_lo), core: 2. Of those that a mesh axis runs over, the one named last changes fastest.
Arguments:
- view_one: bfloat16 [4096, 8192], P('row', 'col'), may hold values from -6 to 6
- view_two: bfloat16 [4096, 8192], P('row', 'col'), may hold values from -6 to 6
- pair_weights: bfloat16 [8192, 8192], P('row', 'col'), may hold values from 0.25 to 2.5
Outputs:
- first_grad: bfloat16 [4096, 8192], P('row', 'col')
- second_grad: bfloat16 [4096, 8192], P('row', 'col')
All inputs are finite; a program needn't handle non-finite values.
Results may differ from a plain program's by a relative error of at most 0.004.
Values may be sent and summed in bfloat16 or wider, within the bound.
A program may use at most 128 MiB of HBM per device.

v0:
```python
import jax
import jax.numpy as jnp
from jax import lax
from jax.sharding import Mesh
from jax.sharding import PartitionSpec as P

ROW = ("row_0", "row_1")


def whole_of(array, axes, dim):
    filled = array
    for number in range(len(axes) - 1, -1, -1):
        filled = lax.all_gather(filled, axes[number], axis=dim, tiled=True)
    return filled


def per_device(view_one, view_two, pair_weights):
    wide_two = lax.all_gather(view_two, "col", axis=1, tiled=True)
    samples = view_one.shape[0] * lax.axis_size(ROW)
    local_rows = pair_weights.shape[0]
    local_cols = pair_weights.shape[1]
    regrouped = lax.all_to_all(wide_two, ROW, split_axis=1, concat_axis=0, tiled=True)
    summed = lax.dot_general(
        regrouped,
        lax.all_gather(view_one, ROW, axis=0, tiled=True),
        (((0,), (0,)), ((), ())),
        preferred_element_type=jnp.float32,
    )
    correlation = summed / samples
    row_ids = lax.axis_index(ROW) * local_rows + lax.broadcasted_iota(
        jnp.int32, (local_rows, local_cols), 0
    )
    col_ids = lax.axis_index("col") * local_cols + lax.broadcasted_iota(
        jnp.int32, (local_rows, local_cols), 1
    )
    identity = jnp.where(row_ids == col_ids, 1.0, 0.0).astype(jnp.float32)
    weighted = (pair_weights.astype(jnp.float32) * (correlation - identity)).astype(jnp.bfloat16)
    grad_cols = whole_of(weighted, ROW, 0)
    first_grad = jnp.dot(wide_two, grad_cols, preferred_element_type=jnp.float32).astype(
        jnp.bfloat16
    )
    second_flipped = lax.psum_scatter(
        lax.dot_general(
            grad_cols, view_one, (((1,), (1,)), ((), ())), preferred_element_type=jnp.float32
        ),
        "col",
        scatter_dimension=0,
        tiled=True,
    )
    return (first_grad, second_flipped.T.astype(jnp.bfloat16))


def solution(mesh):
    torus = Mesh(mesh.devices.reshape(4, 2, mesh.shape["col"]), ("row_0", "row_1", "col"))
    placed = (P(ROW, "col"), P(ROW, "col"), P(ROW, "col"))
    return jax.shard_map(
        per_device,
        mesh=torus,
        in_specs=placed,
        out_specs=(P(ROW, "col"), P(ROW, "col")),
        check_vma=False,
    )
```

profile of v0, /device:TPU:0, one launch (start us, length us, event | category | flops | bytes accessed | tf_op | source)
XLA Modules:
  0.0 564.2 jit_solution(15220778001072842064)
XLA Ops:
  8.0 0.0 all-gather.5.cloned.1.call-start
  8.0 2.0 copy.9
  10.1 0.0 all-gather.5.cloned.1.call-update
  10.1 77.0 %all-gather.5.cloned.1.call-done = bf16[512,8192]{0,1:T(8,128)(2,1)} async-done(((bf16[512,512]{0,1:T(8,128)(2,1)}), bf16[512,8192]{0,1:T(8,128)(2,1)}) %all-gather.5.cloned.1.call-update) | async-done | bytes 8388624 | tf_op jit(solution)/shard_map/all_gather | solution.py:18
  87.1 5.0 all-to-all-start
  92.1 0.0 all-gather.7.cloned.1.call-start
  92.2 0.5 all-gather.7.cloned.1.call-update
  92.7 0.0 all-gather.9.cloned.1.call-start
  92.8 125.2 %all-to-all-done = bf16[512,8,1024]{0,2,1:T(8,128)(2,1)} async-done(((bf16[512,8,1024]{0,2,1:T(8,128)(2,1)}), bf16[512,8,1024]{0,2,1:T(8,128)(2,1)}, u32[]{:S(2)}, u32[]{:S(2)}) %all-to-all-start) | async-done | bytes 8388640 | tf_op jit(solution)/shard_map/all_to_all | solution.py:22
  218.0 0.0 copy-start.1
  218.0 11.6 %copy.10 = bf16[8,512,1024]{2,1,0:T(8,128)(2,1)} copy(bf16[8,512,1024]{1,2,0:T(8,128)(2,1)} %bitcast.1) | data formatting | bytes 16777216 | tf_op jit(solution)/shard_map/all_to_all | solution.py:22
  229.6 34.8 %all-gather.7.cloned.1.call-done = bf16[4096,512]{1,0:T(8,128)(2,1)} async-done(((bf16[512,512]{1,0:T(8,128)(2,1)}), bf16[4096,512]{1,0:T(8,128)(2,1)}) %all-gather.7.cloned.1.call-update) | async-done | bytes 4194320 | tf_op jit(solution)/shard_map/all_gather | solution.py:25
  264.4 0.0 copy-done.1
  264.4 0.0 copy-start
  264.4 10.4 %multiply_convert_fusion = bf16[1024,512]{1,0:T(8,128)(2,1)} fusion(bf16[1024,512]{1,0:T(8,128)(2,1)S(1)} %copy-done.1, bf16[4096,1024]{1,0:T(8,128)(2,1)} %bitcast.14, bf16[4096,512]{1,0:T(8,128)(2,1)} %all-gather.7.cloned.1.call-done, s32[512]{0:T(512)S(1)} %iota_add_fusion.1, s32[1024]{0:T(1024)S(1)} %iota_add_fusion), kind=kOutput, calls=%fused_computation | convolution fusion | flops 4298637312 | bytes 14686208 | tf_op jit(solution)/shard_map/dot_general | solution.py:23
  274.8 0.0 all-gather.9.cloned.1.call-update
  274.8 0.0 all-gather.11.cloned.1.call-start
  274.8 34.0 %all-gather.9.cloned.1.call-done = bf16[2048,512]{1,0:T(8,128)(2,1)} async-done(((bf16[1024,512]{1,0:T(8,128)(2,1)}), bf16[2048,512]{1,0:T(8,128)(2,1)}) %all-gather.9.cloned.1.call-update) | async-done | bytes 2097168 | tf_op jit(solution)/shard_map/all_gather | solution.py:13
  308.8 0.0 all-gather.11.cloned.1.call-update
  308.8 0.0 reduce-scatter.2.cloned.1.call-start
  308.9 85.4 %all-gather.11.cloned.1.call-done = bf16[8192,512]{1,0:T(8,128)(2,1)} async-done(((bf16[2048,512]{1,0:T(8,128)(2,1)}), bf16[8192,512]{1,0:T(8,128)(2,1)}) %all-gather.11.cloned.1.call-update) | async-done | bytes 8388624 | tf_op jit(solution)/shard_map/all_gather | solution.py:13
  394.3 0.0 copy-done
  394.3 11.7 %fusion.1 = f32[8192,512]{1,0:T(8,128)} fusion(bf16[8192,512]{1,0:T(8,128)(2,1)} %all-gather.11.cloned.1.call-done, bf16[512,512]{1,0:T(8,128)(2,1)S(1)} %copy-done), kind=kOutput, calls=%fused_computation.6 | convolution fusion | flops 4294967296 | bytes 25690112 | tf_op jit(solution)/shard_map/dot_general | solution.py:43
  405.9 0.0 reduce-scatter.2.cloned.1.call-update
  406.0 10.3 %fusion = bf16[512,512]{0,1:T(8,128)(2,1)S(1)} fusion(bf16[8192,512]{1,0:T(8,128)(2,1)} %all-gather.11.cloned.1.call-done, bf16[512,8192]{0,1:T(8,128)(2,1)} %all-gather.5.cloned.1.call-done), kind=kOutput, calls=%fused_computation.2 | convolution fusion | flops 4295229440 | bytes 17301504 | tf_op jit(solution)/shard_map/dot_general | solution.py:39
  416.2 1.0 copy.11
  417.2 137.1 %reduce-scatter.2.cloned.1.call-done = f32[512,512]{1,0:T(8,128)} async-done(((f32[8192,512]{1,0:T(8,128)}), f32[512,512]{1,0:T(8,128)}) %reduce-scatter.2.cloned.1.call-update) | async-done | bytes 1048592 | tf_op jit(solution)/shard_map/reduce_scatter | solution.py:42
  554.3 1.3 convert_bitcast_fusion
  555.6 1.0 copy.12
  (2 shorter events, 0.0 us)
Async XLA Ops:
  8.0 79.1 %all-gather.5.cloned.1.call-start = ((), (), s32[]{:S(2)}) async-start(), calls=%async_computation.2 | async-start | bytes 8912896 | tf_op jit(solution)/shard_map/all_gather | solution.py:18
  87.1 130.9 %all-to-all-start = ((bf16[512,8,1024]{0,2,1:T(8,128)(2,1)}), bf16[512,8,1024]{0,2,1:T(8,128)(2,1)}, u32[]{:S(2)}, u32[]{:S(2)}) async-start(bf16[512,8,1024]{0,2,1:T(8,128)(2,1)} %bitcast.13), calls=%async_computation | async-start | bytes 16777216 | tf_op jit(solution)/shard_map/all_to_all | solution.py:22
  92.1 172.3 %all-gather.7.cloned.1.call-start = ((), (), s32[]{:S(2)}) async-start(), calls=%async_computation.3 | async-start | bytes 4718592 | tf_op jit(solution)/shard_map/all_gather | solution.py:25
  92.7 216.1 %all-gather.9.cloned.1.call-start = ((), (), s32[]{:S(2)}) async-start(), calls=%async_computation.4 | async-start | bytes 3145728 | tf_op jit(solution)/shard_map/all_gather | solution.py:13
  218.0 46.4 %copy-start.1 = (bf16[1024,512]{1,0:T(8,128)(2,1)S(1)}, bf16[1024,512]{1,0:T(8,128)(2,1)}, u32[]{:S(2)}) copy-start(bf16[1024,512]{1,0:T(8,128)(2,1)} %param.5) | copy-start | bytes 3145732
  264.4 129.9 %copy-start = (bf16[512,512]{1,0:T(8,128)(2,1)S(1)}, bf16[512,512]{1,0:T(8,128)(2,1)}, u32[]{:S(2)}) copy-start(bf16[512,512]{1,0:T(8,128)(2,1)} %param.3) | copy-start | bytes 1572868
  274.8 119.5 %all-gather.11.cloned.1.call-start = ((), (), s32[]{:S(2)}) async-start(), calls=%async_computation.5 | async-start | bytes 10485760 | tf_op jit(solution)/shard_map/all_gather | solution.py:13
  308.8 245.5 %reduce-scatter.2.cloned.1.call-start = ((), (), s32[]{:S(2)}) async-start(), calls=%async_computation.6 | async-start | bytes 17825792 | tf_op jit(solution)/shard_map/reduce_scatter | solution.py:42
Sparse Core Ops, SparseCore 0:
  11.8 75.2 all-gather.4
  406.1 148.1 reduce-scatter.1
Sparse Core Ops, SparseCore 1:
  94.2 170.1 all-gather.6
  274.9 33.9 all-gather.8
  310.3 83.9 all-gather.10
where the time goes:
time: 565 us; the launch traced here: 564 us
  waiting for transfers between devices  494 us (87%)
  matrix products  32.3 us (6%)
  local copies, waits for them, and re-layouts  15.7 us (3%)
  between operations  15.7 us (3%)
    reduce_scatter x1, waiting for transfers between devices, per_device(): lax.psum_scatter(lax.dot_general(grad_cols, view_one, (((1,), (1,)), ((),...  137 us
    all_to_all x1, waiting for transfers between devices, per_device(): lax.all_to_all(wide_two, ROW, split_axis=1, concat_axis=0, tiled=True)  125 us
    all_gather x2, waiting for transfers between devices, whole_of(): filled = lax.all_gather(filled, axes[number], axis=dim, tiled=True)  119 us
    all_gather x1, waiting for transfers between devices, per_device(): wide_two = lax.all_gather(view_two, 'col', axis=1, tiled=True)  77 us
    all_gather x1, waiting for transfers between devices, per_device(): lax.all_gather(view_one, ROW, axis=0, tiled=True)  34.8 us
    dot_general x1, matrix products, per_device(): lax.dot_general(grad_cols, view_one, (((1,), (1,)), ((), ())), preferred_...  11.7 us
    all_to_all x1, local copies, waits for them, and re-layouts, per_device(): lax.all_to_all(wide_two, ROW, split_axis=1, concat_axis=0, tiled=True)  11.6 us
  transfers between devices with their start and end apart: 6, of which 6 were waited for; matrix products, arithmetic and copies ran while one was open for 4% of the time, Pallas kernels for 0%

commit v1 on v0

--- a/solution.py
+++ b/solution.py
@@ -19,7 +19,10 @@
     samples = view_one.shape[0] * lax.axis_size(ROW)
     local_rows = pair_weights.shape[0]
     local_cols = pair_weights.shape[1]
-    regrouped = lax.all_to_all(wide_two, ROW, split_axis=1, concat_axis=0, tiled=True)
+    regrouped = jnp.concatenate(
+        lax.all_to_all(jnp.stack(jnp.split(wide_two, lax.axis_size(ROW), axis=1)), ROW, 0, 0),
+        axis=0,
+    )
     summed = lax.dot_general(
         regrouped,
         lax.all_gather(view_one, ROW, axis=0, tiled=True),

time: 565 us -> 574 us (1.016)
  waiting for transfers between devices: 494 us -> 500 us
    all_to_all x1, waiting for transfers between devices: 125 us -> 0.01 us  [per_device(): lax.all_to_all(jnp.stack(jnp.split(wide_two, lax.axis_size(ROW), axis=1))...]
    all_gather x1, waiting for transfers between devices: 34.8 us -> 156 us  [per_device(): lax.all_gather(view_one, ROW, axis=0, tiled=True)]
    unnamed x7 -> x13, local copies, waits for them, and re-layouts: 4.06 us -> 18.1 us
    all_to_all x1 -> x0, local copies, waits for them, and re-layouts: 11.6 us -> none  [per_device(): lax.all_to_all(wide_two, ROW, split_axis=1, concat_axis=0, tiled=True)]
    all_gather x1, waiting for transfers between devices: 77 us -> 83.3 us  [per_device(): wide_two = lax.all_gather(view_two, 'col', axis=1, tiled=True)]
  transfers between devices with their start and end apart: 6 -> 6, of which waited for: 6 -> 5; matrix products, arithmetic and copies ran while one was open for 4% -> 5% of each run, Pallas kernels for 0% -> 0%
where the time goes in v1:
time: 574 us; the launch traced here: 573 us
  waiting for transfers between devices  500 us (87%)
  matrix products  32.3 us (6%)
  local copies, waits for them, and re-layouts  20.4 us (4%)
  between operations  13.8 us (2%)
    all_gather x1, waiting for transfers between devices, per_device(): lax.all_gather(view_one, ROW, axis=0, tiled=True)  156 us
    reduce_scatter x1, waiting for transfers between devices, per_device(): lax.psum_scatter(lax.dot_general(grad_cols, view_one, (((1,), (1,)), ((),...  137 us
    all_gather x2, waiting for transfers between devices, whole_of(): filled = lax.all_gather(filled, axes[number], axis=dim, tiled=True)  122 us
    all_gather x1, waiting for transfers between devices, per_device(): wide_two = lax.all_gather(view_two, 'col', axis=1, tiled=True)  83.3 us
    unnamed x13, local copies, waits for them, and re-layouts  18.1 us
    dot_general x1, matrix products, per_device(): lax.dot_general(grad_cols, view_one, (((1,), (1,)), ((), ())), preferred_...  11.7 us
  transfers between devices with their start and end apart: 6, of which 5 were waited for; matrix products, arithmetic and copies ran while one was open for 5% of the time, Pallas kernels for 0%

profile of v1, /device:TPU:0, one launch (start us, length us, event | category | flops | bytes accessed | tf_op | source)
XLA Modules:
  0.0 573.1 jit_solution(801182867494010707)
XLA Ops:
  7.2 0.0 all-gather.5.cloned.1.call-start
  7.2 0.7 all-gather.5.cloned.1.call-update
  7.9 0.0 all-gather.7.cloned.1.call-start
  7.9 0.7 all-gather.7.cloned.1.call-update
  8.6 83.3 %all-gather.5.cloned.1.call-done = bf16[512,8192]{1,0:T(8,128)(2,1)} async-done(((bf16[512,512]{1,0:T(8,128)(2,1)}), bf16[512,8192]{1,0:T(8,128)(2,1)}) %all-gather.5.cloned.1.call-update) | async-done | bytes 8388624 | tf_op jit(solution)/shard_map/all_gather | solution.py:18
  91.9 2.4 fusion.8
  94.3 2.3 fusion.7
  96.6 2.3 fusion.6
  98.8 2.3 fusion.5
  101.1 2.3 fusion.4
  103.5 2.3 fusion.3
  105.7 2.3 fusion.2
  108.0 2.3 fusion.1
  110.3 0.0 copy-start.1
  110.3 5.1 all-to-all-start
  115.4 0.0 all-gather.9.cloned.1.call-start
  115.4 156.0 %all-gather.7.cloned.1.call-done = bf16[4096,512]{1,0:T(8,128)(2,1)} async-done(((bf16[512,512]{1,0:T(8,128)(2,1)}), bf16[4096,512]{1,0:T(8,128)(2,1)}) %all-gather.7.cloned.1.call-update) | async-done | bytes 4194320 | tf_op jit(solution)/shard_map/all_gather | solution.py:28
  271.5 0.0 all-to-all-done
  271.5 0.0 copy-done.1
  271.5 0.0 copy-start
  271.5 10.4 %multiply_convert_fusion = bf16[1024,512]{1,0:T(8,128)(2,1)} fusion(bf16[1024,512]{1,0:T(8,128)(2,1)S(1)} %copy-done.1, bf16[4096,1024]{1,0:T(8,128)(2,1)} %bitcast.8, bf16[4096,512]{1,0:T(8,128)(2,1)} %all-gather.7.cloned.1.call-done, s32[512]{0:T(512)S(1)} %iota_add_fusion.1, s32[1024]{0:T(1024)S(1)} %iota_add_fusion), kind=kOutput, calls=%fused_computation | convolution fusion | flops 4298637312 | bytes 14686208 | tf_op jit(solution)/shard_map/dot_general | solution.py:26
  281.8 0.0 all-gather.9.cloned.1.call-update
  281.9 0.0 all-gather.11.cloned.1.call-start
  281.9 36.7 %all-gather.9.cloned.1.call-done = bf16[2048,512]{1,0:T(8,128)(2,1)} async-done(((bf16[1024,512]{1,0:T(8,128)(2,1)}), bf16[2048,512]{1,0:T(8,128)(2,1)}) %all-gather.9.cloned.1.call-update) | async-done | bytes 2097168 | tf_op jit(solution)/shard_map/all_gather | solution.py:13
  318.6 0.0 all-gather.11.cloned.1.call-update
  318.7 0.2 reduce-scatter.2.cloned.1.call-start
  318.9 85.4 %all-gather.11.cloned.1.call-done = bf16[8192,512]{1,0:T(8,128)(2,1)} async-done(((bf16[2048,512]{1,0:T(8,128)(2,1)}), bf16[8192,512]{1,0:T(8,128)(2,1)}) %all-gather.11.cloned.1.call-update) | async-done | bytes 8388624 | tf_op jit(solution)/shard_map/all_gather | solution.py:13
  404.2 0.0 copy-done
  404.2 11.7 %fusion.9 = f32[8192,512]{1,0:T(8,128)} fusion(bf16[8192,512]{1,0:T(8,128)(2,1)} %all-gather.11.cloned.1.call-done, bf16[512,512]{1,0:T(8,128)(2,1)S(1)} %copy-done), kind=kOutput, calls=%fused_computation.22 | convolution fusion | flops 4294967296 | bytes 25690112 | tf_op jit(solution)/shard_map/dot_general | solution.py:46
  415.9 0.0 reduce-scatter.2.cloned.1.call-update
  415.9 10.3 %fusion = bf16[512,512]{0,1:T(8,128)(2,1)S(1)} fusion(bf16[8192,512]{1,0:T(8,128)(2,1)} %all-gather.11.cloned.1.call-done, bf16[512,8192]{1,0:T(8,128)(2,1)} %all-gather.5.cloned.1.call-done), kind=kOutput, calls=%fused_computation.2 | convolution fusion | flops 4295229440 | bytes 17301504 | tf_op jit(solution)/shard_map/dot_general | solution.py:42
  426.2 1.0 copy.5
  427.2 137.1 %reduce-scatter.2.cloned.1.call-done = f32[512,512]{1,0:T(8,128)} async-done(((f32[8192,512]{1,0:T(8,128)}), f32[512,512]{1,0:T(8,128)}) %reduce-scatter.2.cloned.1.call-update) | async-done | bytes 1048592 | tf_op jit(solution)/shard_map/reduce_scatter | solution.py:45
  564.3 1.3 convert_bitcast_fusion
  565.6 1.0 copy.6
  (2 shorter events, 0.0 us)
Async XLA Ops:
  7.2 84.8 %all-gather.5.cloned.1.call-start = ((), (), s32[]{:S(2)}) async-start(), calls=%async_computation.2 | async-start | bytes 8912896 | tf_op jit(solution)/shard_map/all_gather | solution.py:18
  7.9 263.6 %all-gather.7.cloned.1.call-start = ((), (), s32[]{:S(2)}) async-start(), calls=%async_computation.3 | async-start | bytes 4718592 | tf_op jit(solution)/shard_map/all_gather | solution.py:28
  110.3 161.2 %copy-start.1 = (bf16[1024,512]{1,0:T(8,128)(2,1)S(1)}, bf16[1024,512]{1,0:T(8,128)(2,1)}, u32[]{:S(2)}) copy-start(bf16[1024,512]{1,0:T(8,128)(2,1)} %param.5) | copy-start | bytes 3145732
  110.3 161.2 %all-to-all-start = ((bf16[8,512,1024]{2,1,0:T(8,128)(2,1)}), bf16[8,512,1024]{2,1,0:T(8,128)(2,1)}, u32[]{:S(2)}, u32[]{:S(2)}) async-start(bf16[8,512,1024]{2,1,0:T(8,128)(2,1)} %fusion.1), calls=%async_computation | async-start | bytes 16777216 | tf_op jit(solution)/shard_map/all_to_all | solution.py:23
  115.4 203.3 %all-gather.9.cloned.1.call-start = ((), (), s32[]{:S(2)}) async-start(), calls=%async_computation.4 | async-start | bytes 3145728 | tf_op jit(solution)/shard_map/all_gather | solution.py:13
  271.5 132.8 %copy-start = (bf16[512,512]{1,0:T(8,128)(2,1)S(1)}, bf16[512,512]{1,0:T(8,128)(2,1)}, u32[]{:S(2)}) copy-start(bf16[512,512]{1,0:T(8,128)(2,1)} %param.3) | copy-start | bytes 1572868
  281.9 122.4 %all-gather.11.cloned.1.call-start = ((), (), s32[]{:S(2)}) async-start(), calls=%async_computation.5 | async-start | bytes 10485760 | tf_op jit(solution)/shard_map/all_gather | solution.py:13
  318.7 245.6 %reduce-scatter.2.cloned.1.call-start = ((), (), s32[]{:S(2)}) async-start(), calls=%async_computation.6 | async-start | bytes 17825792 | tf_op jit(solution)/shard_map/reduce_scatter | solution.py:45
Sparse Core Ops, SparseCore 0:
  10.2 81.6 all-gather.4
  93.6 177.8 all-gather.6
  282.0 36.6 all-gather.8
  320.2 84.0 all-gather.10
  416.0 148.2 reduce-scatter.1
